TPU v7x, 32 devices: a whole 2x2x4 slice. The times are simulated.
32 devices in a mesh: row: 8 (over z, x), col: 4 (over y, core).
Axes of the slice: x: 2, y: 2, z: 4, core: 2. Of those that a mesh axis runs over, the one named last changes fastest.
Arguments:
- gradients: bfloat16 [8, 4, 4, 64, 1536], P('row', 'col'), may hold values from -96 to 96
- token_counts: int32 [8, 4], P('row', 'col'), may hold values from 16 to 256
- row_groups: int32 [2, 8, 4], replicated, may hold values from 0 to 3, each once within a row
- col_groups: int32 [1, 4, 8], replicated, may hold values from 0 to 7, each once within a row
Outputs:
- averaged: float32 [8, 4, 4, 64, 1536], P('row', 'col')
- totals: int32 [8, 4], P('row', 'col')
Inputs may be any that keep to these rules, and one draw needn't show every extreme that they name: row_groups[r, i] lists the 4 grid columns in some order: in row round r, grid row i's member of group g sits in column row_groups[r, i, g]. col_groups[0, j] lists the 8 grid rows in some order: grid column j's member of group h sits in row col_groups[0, j, h].
All inputs are finite; a program needn't handle non-finite values.
Results may differ from a plain program's by a relative error of at most 0.0003.
Values may be sent and summed in bfloat16 or wider, within the bound.
A program may use at most 64 MiB of HBM per device.

v0:
```python
import jax
import jax.numpy as jnp
from jax import lax
from jax.sharding import PartitionSpec as P


def weigh_groups(pieces, weights, group_order):
    scaled = pieces * weights[:, None, None]
    return (jnp.take(scaled, group_order, axis=0), jnp.take(weights, group_order, axis=0))


def return_order(averaged, weights, group_order):
    inverse = jnp.argsort(group_order)
    return (jnp.take(averaged, inverse, axis=0), jnp.take(weights, inverse, axis=0))


def opening_spread(gradients, weight):
    members = lax.axis_size("col")
    pieces = gradients.reshape(members, -1, gradients.shape[-1])
    spread = jnp.full((members,), weight, jnp.float32).astype(jnp.bfloat16)
    arrived, arrived_w = (
        lax.all_to_all(pieces, "col", split_axis=0, concat_axis=0, tiled=True),
        lax.all_to_all(spread, "col", split_axis=0, concat_axis=0, tiled=True),
    )
    return (arrived.astype(jnp.float32), arrived_w.astype(jnp.float32))


def regroup(values, weights, index_table):
    groups = values.shape[0]
    selector = (
        index_table[:, :, None] == jnp.arange(groups, dtype=jnp.int32)[None, None, :]
    ).astype(jnp.float32)
    mixing = jnp.sum(selector, axis=1) * weights[None, :]
    flattened = values.reshape(groups, -1)
    numerator = jnp.dot(
        mixing, flattened, precision=lax.Precision.HIGHEST, preferred_element_type=jnp.float32
    )
    new_totals = jnp.sum(mixing, axis=1)
    mixed = numerator / new_totals[:, None]
    return (mixed.reshape((index_table.shape[0],) + values.shape[1:]), new_totals)


def local(gradients, token_counts, row_groups, col_groups):
    row_place = lax.axis_index("row")
    state_shape = (gradients.shape[2] * gradients.shape[3], gradients.shape[4])
    weight = token_counts.reshape(()).astype(jnp.float32)
    arrived, arrived_w = opening_spread(gradients, weight)
    members = lax.axis_size("col")
    row_count = lax.axis_size("row")
    ordered, group_w = weigh_groups(arrived, arrived_w, row_groups[0, row_place])
    first_inverse = jnp.argsort(row_groups[0], axis=1)
    column_ids = jnp.arange(members, dtype=jnp.int32)
    index_two = first_inverse[col_groups[0].T, column_ids[None, :]]
    second_inverse = jnp.argsort(col_groups[0], axis=1)
    row_ids = jnp.arange(row_count, dtype=jnp.int32)
    index_three = second_inverse[row_groups[1].T, row_ids[None, :]]
    group_sums, first_w = lax.psum((ordered, group_w), "row")
    first_avg = group_sums / first_w[:, None, None]
    second, second_w = regroup(first_avg, first_w, index_two)
    third_avg, third_w = regroup(second, second_w, index_three)
    outgoing, outgoing_w = return_order(third_avg, third_w, row_groups[1, row_place])
    returned, returned_w = (
        lax.all_to_all(outgoing, "col", split_axis=0, concat_axis=0, tiled=True),
        lax.all_to_all(outgoing_w, "col", split_axis=0, concat_axis=0, tiled=True),
    )
    grad_state = returned.reshape(state_shape)
    weight = returned_w[0]
    return (
        grad_state.reshape(gradients.shape),
        weight.astype(jnp.int32).reshape(token_counts.shape),
    )


def solution(mesh):
    placed = (P("row", "col", None, None, None), P("row", "col"), P(), P())
    return jax.shard_map(
        local,
        mesh=mesh,
        in_specs=placed,
        out_specs=(P("row", "col", None, None, None), P("row", "col")),
        check_vma=False,
    )
```

profile of v0, /device:TPU:0, one launch (start us, length us, event | category | flops | bytes accessed | tf_op | source)
XLA Modules:
  0.0 169.0 jit_solution(17245745571147319791)
XLA Ops:
  7.8 0.6 broadcast_in_dim.26
  8.4 4.3 %all-to-all-start = ((bf16[4,1,1]{2,1,0:T(2,128)(2,1)}), bf16[4,1,1]{2,1,0:T(2,128)(2,1)S(1)}, u32[]{:S(2)}, u32[]{:S(2)}) async-start(bf16[4,1,1]{2,1,0:T(2,128)(2,1)} %broadcast_in_dim.26), calls=%async_computation | async-start | bytes 4096 | tf_op jit(solution)/shard_map/all_to_all | solution.py:23
  12.7 0.9 dynamic-slice_reduce_fusion
  13.6 2.8 %all-to-all-done = bf16[4,1,1]{2,1,0:T(2,128)(2,1)S(1)} async-done(((bf16[4,1,1]{2,1,0:T(2,128)(2,1)}), bf16[4,1,1]{2,1,0:T(2,128)(2,1)S(1)}, u32[]{:S(2)}, u32[]{:S(2)}) %all-to-all-start) | async-done | bytes 40 | tf_op jit(solution)/shard_map/all_to_all | solution.py:23
  16.4 3.5 %all-to-all-start.1 = ((bf16[4,64,1536]{2,1,0:T(8,128)(2,1)}), bf16[4,64,1536]{2,1,0:T(8,128)(2,1)S(1)}, u32[]{:S(2)}, u32[]{:S(2)}) async-start(bf16[4,64,1536]{2,1,0:T(8,128)(2,1)} %bitcast.41), calls=%async_computation.1 | async-start | bytes 1572864 | tf_op jit(solution)/shard_map/all_to_all | solution.py:22
  19.9 0.0 all-reduce.2.cloned.1.call-start
  19.9 0.1 convert_reduce_fusion.2
  20.1 0.6 gather_fusion.2
  20.7 10.7 %all-to-all-done.1 = bf16[4,64,1536]{2,1,0:T(8,128)(2,1)S(1)} async-done(((bf16[4,64,1536]{2,1,0:T(8,128)(2,1)}), bf16[4,64,1536]{2,1,0:T(8,128)(2,1)S(1)}, u32[]{:S(2)}, u32[]{:S(2)}) %all-to-all-start.1) | async-done | bytes 786464 | tf_op jit(solution)/shard_map/all_to_all | solution.py:22
  31.5 0.2 convert_multiply_fusion
  31.7 0.7 gather_fusion.3
  32.4 1.4 broadcast_select_fusion.1
  33.8 0.0 copy-start.1
  33.8 0.0 all-reduce.2.cloned.1.call-update
  33.8 0.7 copy-done.1
  34.5 0.1 copy.20
  34.6 0.1 reshape.95
  34.6 0.0 copy-done
  34.7 0.6 sort.52
  35.3 0.8 gather_fusion.1
  36.0 0.1 reshape.98
  36.1 0.1 copy.21
  36.2 0.1 copy.19
  36.3 0.1 reshape.89
  36.4 0.7 sort.51
  37.0 0.7 gather_fusion
  37.7 0.1 reshape.92
  37.8 0.8 sort.53
  38.6 0.1 convert_reduce_fusion
  38.7 22.8 %psum.14 = f32[4]{0:T(128)S(1)} all-reduce(f32[4]{0:T(128)S(1)} %get-tuple-element.14), channel_id=1, replica_groups=mesh['row'=8,'col'=4] {'row'}, use_global_device_ids=true, to_apply=%region_4.6 | all-reduce | flops 4 | bytes 32 | tf_op jit(solution)/shard_map/psum | solution.py:57
  61.5 0.1 multiply_reduce_fusion.1
  61.5 0.1 multiply_reduce_fusion
  61.7 0.6 gather_fusion.5
  62.3 0.7 copy.22
  63.0 3.2 %all-to-all-start.3 = ((f32[4,1,1]{2,1,0:T(1,128)}), f32[4,1,1]{2,1,0:T(1,128)S(1)}, u32[]{:S(2)}, u32[]{:S(2)}) async-start(f32[4,1,1]{2,1,0:T(1,128)} %copy.22), calls=%async_computation.3 | async-start | bytes 4096 | tf_op jit(solution)/shard_map/all_to_all | solution.py:64
  66.2 58.1 %all-reduce.2.cloned.1.call-done = f32[4,64,1536]{2,1,0:T(8,128)} async-done(((f32[4,64,1536]{2,1,0:T(8,128)}), f32[4,64,1536]{2,1,0:T(8,128)}) %all-reduce.2.cloned.1.call-update) | async-done | bytes 1572880 | tf_op jit(solution)/shard_map/psum | solution.py:57
  124.3 1.6 divide_bitcast_fusion
  125.9 1.0 copy.23
  127.0 3.9 %convolution_divide_fusion = f32[8,98304]{1,0:T(8,128)S(1)} fusion(f32[4,98304]{1,0:T(4,128)S(1)} %bitcast.40, f32[8]{0:T(128)S(1)} %multiply_reduce_fusion.1, f32[8,4]{0,1:T(4,128)S(1)} %convert_reduce_fusion.1, f32[4]{0:T(128)S(1)} %psum.14), kind=kOutput, calls=%fused_computation.6 | convolution fusion | flops 38535200 | bytes 4718768 | tf_op jit(solution)/shard_map/dot_general | solution.py:35
  130.9 2.8 %convolution_divide_fusion.1 = f32[4,98304]{1,0:T(4,128)S(1)} fusion(f32[8,98304]{1,0:T(8,128)S(1)} %convolution_divide_fusion, f32[4]{0:T(128)S(1)} %multiply_reduce_fusion, f32[4,8]{1,0:T(4,128)S(1)} %convert_reduce_fusion, f32[8]{0:T(128)S(1)} %multiply_reduce_fusion.1), kind=kOutput, calls=%fused_computation.7 | convolution fusion | flops 38141984 | bytes 4718768 | tf_op jit(solution)/shard_map/dot_general | solution.py:35
  133.7 0.5 copy.26
  134.2 0.7 gather_fusion.4
  134.9 1.4 broadcast_select_fusion
  136.3 0.0 all-to-all-done.3
  136.3 3.6 %all-to-all-start.2 = ((f32[4,64,1536]{2,1,0:T(8,128)}), f32[4,64,1536]{2,1,0:T(8,128)S(1)}, u32[]{:S(2)}, u32[]{:S(2)}) async-start(f32[4,64,1536]{2,1,0:T(8,128)} %broadcast_select_fusion), calls=%async_computation.2 | async-start | bytes 3145728 | tf_op jit(solution)/shard_map/all_to_all | solution.py:63
  139.9 0.6 slice.25
  141.1 18.7 %all-to-all-done.2 = f32[4,64,1536]{2,1,0:T(8,128)S(1)} async-done(((f32[4,64,1536]{2,1,0:T(8,128)}), f32[4,64,1536]{2,1,0:T(8,128)S(1)}, u32[]{:S(2)}, u32[]{:S(2)}) %all-to-all-start.2) | async-done | bytes 1572896 | tf_op jit(solution)/shard_map/all_to_all | solution.py:63
  159.9 1.1 copy.30
  (14 shorter events, 0.1 us)
Async XLA Ops:
  8.4 8.0 %all-to-all-start = ((bf16[4,1,1]{2,1,0:T(2,128)(2,1)}), bf16[4,1,1]{2,1,0:T(2,128)(2,1)S(1)}, u32[]{:S(2)}, u32[]{:S(2)}) async-start(bf16[4,1,1]{2,1,0:T(2,128)(2,1)} %broadcast_in_dim.26), calls=%async_computation | async-start | bytes 4096 | tf_op jit(solution)/shard_map/all_to_all | solution.py:23
  16.4 15.1 %all-to-all-start.1 = ((bf16[4,64,1536]{2,1,0:T(8,128)(2,1)}), bf16[4,64,1536]{2,1,0:T(8,128)(2,1)S(1)}, u32[]{:S(2)}, u32[]{:S(2)}) async-start(bf16[4,64,1536]{2,1,0:T(8,128)(2,1)} %bitcast.41), calls=%async_computation.1 | async-start | bytes 1572864 | tf_op jit(solution)/shard_map/all_to_all | solution.py:22
  19.9 104.4 %all-reduce.2.cloned.1.call-start = ((), (), s32[]{:S(2)}) async-start(), calls=%async_computation.4 | async-start | bytes 3145728 | tf_op jit(solution)/shard_map/psum | solution.py:57
  33.8 0.7 copy-start.1
  33.8 0.9 copy-start
  63.0 73.3 %all-to-all-start.3 = ((f32[4,1,1]{2,1,0:T(1,128)}), f32[4,1,1]{2,1,0:T(1,128)S(1)}, u32[]{:S(2)}, u32[]{:S(2)}) async-start(f32[4,1,1]{2,1,0:T(1,128)} %copy.22), calls=%async_computation.3 | async-start | bytes 4096 | tf_op jit(solution)/shard_map/all_to_all | solution.py:64
  136.3 23.6 %all-to-all-start.2 = ((f32[4,64,1536]{2,1,0:T(8,128)}), f32[4,64,1536]{2,1,0:T(8,128)S(1)}, u32[]{:S(2)}, u32[]{:S(2)}) async-start(f32[4,64,1536]{2,1,0:T(8,128)} %broadcast_select_fusion), calls=%async_computation.2 | async-start | bytes 3145728 | tf_op jit(solution)/shard_map/all_to_all | solution.py:63
Sparse Core Ops, SparseCore 0:
  33.9 90.3 all-reduce.1
where the time goes:
time: 169 us
  waiting for transfers between devices  90.4 us (53%)
  blocking collectives  22.8 us (13%)
  between operations  16.6 us (10%)
  starting transfers between devices  14.6 us (9%)
  local copies, waits for them, and re-layouts  10.7 us (6%)
  other arithmetic  7.22 us (4%)
  matrix products  6.72 us (4%)
    psum x1, waiting for transfers between devices, local(): group_sums, first_w = lax.psum((ordered, group_w), 'row')  58.1 us
    psum x1, blocking collectives, local(): group_sums, first_w = lax.psum((ordered, group_w), 'row')  22.8 us
    all_to_all x1, waiting for transfers between devices, local(): lax.all_to_all(outgoing, 'col', split_axis=0, concat_axis=0, tiled=True)  18.7 us
    all_to_all x1, waiting for transfers between devices, opening_spread(): lax.all_to_all(pieces, 'col', split_axis=0, concat_axis=0, tiled=True)  10.7 us
    dot_general x2, matrix products, regroup(): jnp.dot(mixing, flattened, precision=lax.Precision.HIGHEST, preferred_ele...  6.72 us
    all_to_all x1, starting transfers between devices, opening_spread(): lax.all_to_all(spread, 'col', split_axis=0, concat_axis=0, tiled=True)  4.26 us
    all_to_all x1, starting transfers between devices, local(): lax.all_to_all(outgoing, 'col', split_axis=0, concat_axis=0, tiled=True)  3.56 us
    all_to_all x1, starting transfers between devices, opening_spread(): lax.all_to_all(pieces, 'col', split_axis=0, concat_axis=0, tiled=True)  3.5 us
  transfers between devices with their start and end apart: 5, of which 4 were waited for; matrix products, arithmetic and copies ran while one was open for 12% of the time, Pallas kernels for 0%

commit v1 on v0

v1 whole, which is shorter than its diff:
```python
import functools

import jax
import jax.numpy as jnp
from jax import lax
from jax.experimental import pallas as pl
from jax.experimental.pallas import tpu as pltpu
from jax.sharding import PartitionSpec as P

MESH = pl.DeviceIdType.MESH
F32 = jnp.float32
SKEW = 2


def path_counts(row_groups, col_groups):
    rows, cols = row_groups.shape[1], row_groups.shape[2]
    row_ids = jnp.arange(rows, dtype=jnp.int32)
    col_ids = jnp.arange(cols, dtype=jnp.int32)
    first = (row_groups[0][:, None, :] == col_ids[None, :, None]).astype(F32)
    last = (row_groups[1][:, None, :] == col_ids[None, :, None]).astype(F32)
    between = (col_groups[0][None, :, :] == row_ids[:, None, None]).astype(F32)
    exact = functools.partial(jnp.einsum, precision=lax.Precision.HIGHEST)
    to_second = exact("ijh,ijg->hg", between, first)
    to_third = exact("ijk,ijh->kh", last, between)
    paths = exact("kh,hg->kg", to_third, to_second)
    coefficient = exact("ijg,kg->ijk", first, paths)
    groups = jnp.arange(cols, dtype=F32)
    chosen = jnp.sum(last * groups[None, None, :], axis=2).astype(jnp.int32)
    return coefficient.reshape(rows * cols, cols), chosen.reshape(rows * cols)


def kernel(
    geometry,
    coef_ref, chosen_ref, count_ref, x_ref,
    out_ref, total_ref,
    recv, own, up_out, up_in, down_out, down_in, tot, ret,
    cnt_send, cnt, part_send, parts, inverse,
    x_send_sem, x_recv_sem, r_send_sem, r_recv_sem, z_send_sem, z_recv_sem,
    c_send_sem, c_recv_sem, p_send_sem, p_recv_sem,
):
    across, cols, depth, chunks, wide, groups = geometry
    plane = across * cols
    row, col = lax.axis_index("row"), lax.axis_index("col")
    z = row // across
    me = (row % across) * cols + col

    def member(q):
        return (z * across + q // cols, q % cols)

    def level(other):
        return (other * across + row % across, col)

    def lanes(k):
        return pl.ds(pl.multiple_of(k * wide, 128), wide)

    barrier = pltpu.get_barrier_semaphore()
    for d in range(1, plane):
        pl.semaphore_signal(barrier, inc=1, device_id=member((me + d) % plane), device_id_type=MESH)
    for d in range(1, depth):
        pl.semaphore_signal(barrier, inc=1, device_id=level((z + d) % depth), device_id_type=MESH)
    count = count_ref[0, 0].astype(F32)
    cnt_send[...] = jnp.full(cnt_send.shape, count, F32)
    cnt[me] = jnp.full(cnt_send.shape, count, F32)
    pl.semaphore_wait(barrier, plane + depth - 2)

    def count_copy(d):
        to = (me + d) % plane
        return pltpu.make_async_remote_copy(
            src_ref=cnt_send, dst_ref=cnt.at[me], send_sem=c_send_sem.at[to], recv_sem=c_recv_sem.at[me],
            device_id=member(to), device_id_type=MESH)

    def count_arrival(q):
        return pltpu.make_async_remote_copy(
            src_ref=cnt_send, dst_ref=cnt.at[q], send_sem=c_send_sem.at[q], recv_sem=c_recv_sem.at[q],
            device_id=member(q), device_id_type=MESH)

    def part_copy(d):
        to = (z + d) % depth
        return pltpu.make_async_remote_copy(
            src_ref=part_send, dst_ref=parts.at[z], send_sem=p_send_sem.at[to], recv_sem=p_recv_sem.at[z],
            device_id=level(to), device_id_type=MESH)

    def part_arrival(s):
        return pltpu.make_async_remote_copy(
            src_ref=part_send, dst_ref=parts.at[s], send_sem=p_send_sem.at[s], recv_sem=p_recv_sem.at[s],
            device_id=level(s), device_id_type=MESH)

    def piece_copy(k, to, slot):
        return pltpu.make_async_remote_copy(
            src_ref=x_ref.at[to, :, lanes(k)], dst_ref=recv.at[k, slot],
            send_sem=x_send_sem.at[k, to], recv_sem=x_recv_sem.at[k, slot],
            device_id=member(to), device_id_type=MESH)

    def result_copy(k, to, slot):
        return pltpu.make_async_remote_copy(
            src_ref=ret.at[k, to], dst_ref=out_ref.at[slot, :, lanes(k)],
            send_sem=r_send_sem.at[k, to], recv_sem=r_recv_sem.at[k, slot],
            device_id=member(to), device_id_type=MESH)

    def result_local(k):
        return pltpu.make_async_copy(ret.at[k, me], out_ref.at[me, :, lanes(k)], r_recv_sem.at[k, me])

    def up_copy(k):
        return pltpu.make_async_remote_copy(
            src_ref=up_out.at[k], dst_ref=up_in.at[k], send_sem=z_send_sem.at[0, k], recv_sem=z_recv_sem.at[0, k],
            device_id=level((z + 1) % depth), device_id_type=MESH)

    def down_copy(k):
        return pltpu.make_async_remote_copy(
            src_ref=down_out.at[k], dst_ref=down_in.at[k], send_sem=z_send_sem.at[1, k], recv_sem=z_recv_sem.at[1, k],
            device_id=level((z + depth - 1) % depth), device_id_type=MESH)

    @pl.loop(1, plane)
    def _(d):
        count_copy(d).start()

    @pl.loop(0, chunks)
    def _(k):
        @pl.loop(1, plane)
        def _(d):
            piece_copy(k, (me + d) % plane, me).start()

    @pl.when(z == 0)
    def _():
        up_in[...] = jnp.zeros(up_in.shape, F32)

    @pl.when(z == depth - 1)
    def _():
        down_in[...] = jnp.zeros(down_in.shape, F32)

    @pl.loop(1, plane)
    def _(d):
        count_arrival((me + d) % plane).wait_recv()

    def factor(q, g):
        return coef_ref[(z * across) * cols + q, g] * cnt[q]

    for g in range(groups):
        part = factor(0, g)
        for q in range(1, plane):
            part = part + factor(q, g)
        part_send[g] = part
        parts[z, g] = part

    @pl.loop(1, depth)
    def _(d):
        part_copy(d).start()

    far = jnp.maximum(z, depth - 1 - z)

    @pl.loop(0, chunks + SKEW * (depth - 1))
    def _(t):
        @pl.when(t < chunks)
        def _():
            recv[t, me] = x_ref[me, :, lanes(t)]

            @pl.loop(1, plane)
            def _(d):
                piece_copy(t, me, (me + d) % plane).wait_recv()

            sums = [None] * groups
            for q in range(plane):
                piece = recv[t, q].astype(F32)
                for g in range(groups):
                    term = piece * factor(q, g)
                    sums[g] = term if q == 0 else sums[g] + term
            for g in range(groups):
                own[t, g] = sums[g]

        up = t - SKEW * z

        @pl.when((up >= 0) & (up < chunks))
        def _():
            @pl.when(z > 0)
            def _():
                up_copy(up).wait_recv()

            @pl.when(z < depth - 1)
            def _():
                up_out[up] = own[up] + up_in[up]
                up_copy(up).start()

        down = t - SKEW * (depth - 1 - z)

        @pl.when((down >= 0) & (down < chunks))
        def _():
            @pl.when(z < depth - 1)
            def _():
                down_copy(down).wait_recv()

            @pl.when(z > 0)
            def _():
                down_out[down] = own[down] + down_in[down]
                down_copy(down).start()

        end = t - SKEW * far

        @pl.when(end == 0)
        def _():
            @pl.loop(1, depth)
            def _(d):
                part_arrival((z + d) % depth).wait_recv()

            for g in range(groups):
                weight = parts[0, g]
                for s in range(1, depth):
                    weight = weight + parts[s, g]
                parts[z, g] = weight
                inverse[g] = 1.0 / weight
            total_ref[...] = parts[z, chosen_ref[row * cols + col]].astype(jnp.int32)

        @pl.when((end >= 0) & (end < chunks))
        def _():
            for g in range(groups):
                tot[g] = (own[end, g] + up_in[end, g] + down_in[end, g]) * inverse[g]

            @pl.loop(1, plane)
            def _(d):
                to = (me + d) % plane
                ret[end, to] = tot[chosen_ref[(z * across) * cols + to]]
                result_copy(end, to, me).start()

            ret[end, me] = tot[chosen_ref[row * cols + col]]
            result_local(end).start()

    @pl.loop(1, plane)
    def _(d):
        count_copy(d).wait_send()

    @pl.loop(1, depth)
    def _(d):
        part_copy(d).wait_send()

    @pl.loop(0, chunks)
    def _(k):
        @pl.when(z < depth - 1)
        def _():
            up_copy(k).wait_send()

        @pl.when(z > 0)
        def _():
            down_copy(k).wait_send()

        @pl.loop(1, plane)
        def _(d):
            piece_copy(k, (me + d) % plane, me).wait_send()
            result_copy(k, (me + d) % plane, me).wait_send()
            result_copy(k, me, (me + d) % plane).wait_recv()

        result_local(k).wait()


def local(gradients, token_counts, row_groups, col_groups):
    rows, cols = lax.axis_size("row"), lax.axis_size("col")
    across = 2 if rows % 2 == 0 else 1
    depth, plane = rows // across, across * cols
    width = gradients.shape[-1]
    height = gradients.size // width // plane
    wide = 256 if width % 256 == 0 else width
    chunks = width // wide
    groups = cols
    coefficient, chosen = path_counts(row_groups, col_groups)
    pieces = gradients.reshape(plane, height, width)
    smem = pl.BlockSpec(memory_space=pltpu.SMEM)
    vmem = pl.BlockSpec(memory_space=pltpu.VMEM)
    slab = pltpu.VMEM((chunks, groups, height, wide), F32)
    sem = pltpu.SemaphoreType.DMA
    averaged, total = pl.pallas_call(
        functools.partial(kernel, (across, cols, depth, chunks, wide, groups)),
        out_shape=(
            jax.ShapeDtypeStruct((plane, height, width), F32),
            jax.ShapeDtypeStruct((1, wide), jnp.int32),
        ),
        in_specs=[smem, smem, smem, vmem],
        out_specs=(pl.BlockSpec(memory_space=pl.ANY), vmem),
        scratch_shapes=[
            pltpu.VMEM((chunks, plane, height, wide), gradients.dtype),
            slab, slab, slab, slab, slab,
            pltpu.VMEM((groups, height, wide), F32),
            pltpu.VMEM((chunks, plane, height, wide), F32),
            pltpu.VMEM((1, wide), F32),
            pltpu.VMEM((plane, 1, wide), F32),
            pltpu.VMEM((groups, 1, wide), F32),
            pltpu.VMEM((depth, groups, 1, wide), F32),
            pltpu.VMEM((groups, 1, wide), F32),
            sem((chunks, plane)), sem((chunks, plane)), sem((chunks, plane)), sem((chunks, plane)),
            sem((2, chunks)), sem((2, chunks)),
            sem((plane,)), sem((plane,)), sem((depth,)), sem((depth,)),
        ],
        compiler_params=pltpu.CompilerParams(
            collective_id=0, has_side_effects=True, vmem_limit_bytes=48 * 1024 * 1024
        ),
    )(coefficient, chosen, token_counts, pieces)
    return averaged.reshape(gradients.shape), total[:, :1]


def solution(mesh):
    placed = (P("row", "col", None, None, None), P("row", "col"), P(), P())
    return jax.shard_map(
        local,
        mesh=mesh,
        in_specs=placed,
        out_specs=(P("row", "col", None, None, None), P("row", "col")),
        check_vma=False,
    )
```

time: 169 us -> 54.3 us (0.32)
  waiting for transfers between devices: 90.4 us -> 0 us
  Pallas kernels: 0 us -> 46.9 us
  blocking collectives: 22.8 us -> 0 us
  between operations: 16.6 us -> 1.3 us
  starting transfers between devices: 14.6 us -> 0 us
  local copies, waits for them, and re-layouts: 10.7 us -> 3.89 us
  other arithmetic: 7.22 us -> 0.73 us
  matrix products: 6.72 us -> 1.33 us
    psum x1 -> x0, waiting for transfers between devices: 58.1 us -> none  [local(): group_sums, first_w = lax.psum((ordered, group_w), 'row')]
    pallas_call x0 -> x1, Pallas kernels: none -> 46.9 us  [local(): pl.pallas_call(functools.partial(kernel, (across, cols, depth, chunks, wi...]
    all_to_all x4 -> x0, waiting for transfers between devices: 32.3 us -> none  [the longest x1 18.7 us: local(): lax.all_to_all(outgoing, 'col', split_axis=0, concat_axis=0, tiled=True)]
    psum x1 -> x0, blocking collectives: 22.8 us -> none  [local(): group_sums, first_w = lax.psum((ordered, group_w), 'row')]
    all_to_all x4 -> x0, starting transfers between devices: 14.5 us -> none  [the longest x1 4.26 us: opening_spread(): lax.all_to_all(spread, 'col', split_axis=0, concat_axis=0, tiled=True)]
    dot_general x2 -> x4, matrix products: 6.72 us -> 1.33 us  [the longest x1 0.87 us: path_counts(): to_second = exact('ijh,ijg->hg', between, first)]
    gather x9 -> x0, local copies, waits for them, and re-layouts: 4.26 us -> none  [the longest x3 0.92 us: local(): index_two = first_inverse[col_groups[0].T, column_ids[None, :]]]
    select_n x5 -> x0, other arithmetic: 2.84 us -> none  [the longest x2 1.42 us: return_order(): jnp.take(averaged, inverse, axis=0)]
  transfers between devices with their start and end apart: 5 -> 0, of which waited for: 4 -> 0; matrix products, arithmetic and copies ran while one was open for 12% -> 0% of each run, Pallas kernels for 0% -> 0%
where the time goes in v1:
time: 54.3 us; the launch traced here: 54.1 us
  Pallas kernels  46.9 us (86%)
  local copies, waits for them, and re-layouts  3.89 us (7%)
  matrix products  1.33 us (2%)
  between operations  1.3 us (2%)
  other arithmetic  0.73 us (1%)
    pallas_call x1, Pallas kernels, local(): pl.pallas_call(functools.partial(kernel, (across, cols, depth, chunks, wi...  46.9 us
    unnamed x3, local copies, waits for them, and re-layouts  2.28 us

profile of v1, /device:TPU:0, one launch (start us, length us, event | category | flops | bytes accessed | tf_op | source)
XLA Modules:
  0.0 54.1 jit_solution(17767084730109659849)
XLA Ops:
  1.3 0.7 %iota_compare_fusion = pred[8,4,8]{2,1,0:T(4,128)(4,1)S(1)} fusion(s32[4,8]{1,0:T(4,128)} %bitcast.21), kind=kLoop, calls=%fused_computation.3 | loop fusion | flops 256 | bytes 384 | tf_op jit(solution)/shard_map/eq | solution.py:21
  2.0 0.7 %slice_bitcast_fusion.1 = (s32[8,4]{0,1:T(4,128)S(1)}, s32[8,4]{0,1:T(4,128)S(1)}) fusion(s32[2,8,4]{1,2,0:T(4,128)} %param.6), kind=kLoop, calls=%fused_computation.10 | loop fusion | bytes 512 | tf_op jit(solution)/shard_map/eq | solution.py:19
  2.7 0.2 convolution_bitcast_fusion.2
  2.9 0.1 copy.13
  3.0 0.9 %convolution_bitcast_fusion.1 = f32[8,4]{0,1:T(4,128)S(1)} fusion(pred[8,4,4]{1,2,0:T(4,128)(4,1)S(1)} %copy.13, s32[4,8]{1,0:T(4,128)} %bitcast.22), kind=kOutput, calls=%fused_computation.1 | convolution fusion | flops 2304 | bytes 384 | tf_op jit(solution)/shard_map/ijh,ijg->hg/dot_general | solution.py:23
  3.9 0.1 convolution_bitcast_fusion
  4.0 0.1 copy.15
  4.1 0.1 convert_element_type.11.chosen_ref
  4.2 0.1 fusion.2
  4.3 0.1 copy.19
  4.4 0.0 copy-start
  4.4 1.1 %copy-done = bf16[1,1,4,64,1536]{4,3,2,1,0:T(8,128)(2,1)S(1)} copy-done((bf16[1,1,4,64,1536]{4,3,2,1,0:T(8,128)(2,1)S(1)}, bf16[1,1,4,64,1536]{4,3,2,1,0:T(8,128)(2,1)}, u32[]{:S(2)}) %copy-start) | copy-done | bytes 786456
  5.6 46.9 %shard_map.59 = (f32[8,32,1536]{2,1,0:T(8,128)S(1)}, s32[1,256]{1,0:T(1,128)S(1)}) custom-call(f32[32,4]{1,0:T(8,128)S(1)} %bitcast.20, s32[32]{0:T(128)S(1)} %convert_element_type.11.chosen_ref, s32[1,1]{1,0:T(1,128)S(6)} %copy.24.count_ref, bf16[8,32,1536]{2,1,0:T(8,128)(2,1)S(1)} %bitcast.19), custom_call_target="tpu_custom_call" | custom-call | tf_op jit(solution)/shard_map/pallas_call | solution.py:268
  52.4 0.5 slice.11
  53.0 1.1 %copy.25 = f32[1,1,4,64,1536]{4,3,2,1,0:T(8,128)} copy(f32[1,1,4,64,1536]{4,3,2,1,0:T(8,128)S(1)} %bitcast.18) | data formatting | bytes 3145728
  (3 shorter events, 0.0 us)
Async XLA Ops:
  4.4 1.1 %copy-start = (bf16[1,1,4,64,1536]{4,3,2,1,0:T(8,128)(2,1)S(1)}, bf16[1,1,4,64,1536]{4,3,2,1,0:T(8,128)(2,1)}, u32[]{:S(2)}) copy-start(bf16[1,1,4,64,1536]{4,3,2,1,0:T(8,128)(2,1)} %param.4) | copy-start | bytes 2359300

commit v2 on v1

--- a/solution.py
+++ b/solution.py
@@ -10,32 +10,75 @@
 MESH = pl.DeviceIdType.MESH
 F32 = jnp.float32
 SKEW = 2
-
-
-def path_counts(row_groups, col_groups):
-    rows, cols = row_groups.shape[1], row_groups.shape[2]
-    row_ids = jnp.arange(rows, dtype=jnp.int32)
-    col_ids = jnp.arange(cols, dtype=jnp.int32)
-    first = (row_groups[0][:, None, :] == col_ids[None, :, None]).astype(F32)
-    last = (row_groups[1][:, None, :] == col_ids[None, :, None]).astype(F32)
-    between = (col_groups[0][None, :, :] == row_ids[:, None, None]).astype(F32)
-    exact = functools.partial(jnp.einsum, precision=lax.Precision.HIGHEST)
-    to_second = exact("ijh,ijg->hg", between, first)
-    to_third = exact("ijk,ijh->kh", last, between)
-    paths = exact("kh,hg->kg", to_third, to_second)
-    coefficient = exact("ijg,kg->ijk", first, paths)
-    groups = jnp.arange(cols, dtype=F32)
-    chosen = jnp.sum(last * groups[None, None, :], axis=2).astype(jnp.int32)
-    return coefficient.reshape(rows * cols, cols), chosen.reshape(rows * cols)
+WIDE = 256
+VMEM_GRANT = 48 * 1024 * 1024
+LIMIT = 32766.0
+FINE = 524200.0
+SMALLEST = 1e-33
+
+
+def path_counts(across, cols, z, table_ref, between_ref, second, third, paths, coef, chosen):
+    hops = between_ref.shape[2]
+
+    def into(turn, h, g):
+        hits = [(table_ref[turn, g, between_ref[0, j, h]] == j).astype(jnp.int32) for j in range(cols)]
+        return functools.reduce(lambda one, two: one + two, hits)
+
+    @pl.loop(0, hops)
+    def _(h):
+        for g in range(cols):
+            second[h, g] = into(0, h, g)
+            third[h, g] = into(1, h, g)
+
+    @pl.loop(0, cols)
+    def _(k):
+        for g in range(cols):
+            paths[k, g] = functools.reduce(
+                lambda one, two: one + two, [third[h, k] * second[h, g] for h in range(hops)])
+
+    @pl.loop(0, across * cols)
+    def _(q):
+        i, j = z * across + q // cols, q % cols
+        mine = last = jnp.int32(0)
+        for g in range(cols):
+            mine = jnp.where(table_ref[0, g, i] == j, g, mine)
+            last = jnp.where(table_ref[1, g, i] == j, g, last)
+        chosen[q] = last
+        for k in range(cols):
+            coef[q, k] = paths[k, mine]
+
+
+def encode(value, k, groups, code_ref, step_ref):
+    for low in range(0, groups, 4):
+        packed = None
+        for g in range(low, min(low + 4, groups)):
+            part = value(g)
+            step = jnp.maximum(jnp.max(jnp.abs(part), axis=0, keepdims=True), SMALLEST) * (1.0 / FINE)
+            step_ref[k, g] = step
+            code = jnp.round(part * (1.0 / step)).astype(jnp.int32)
+            code_ref[k, g] = (code >> 4).astype(jnp.int16)
+            bits = (code & 15) << (4 * (g - low))
+            packed = bits if packed is None else packed + bits
+        code_ref[k, groups + low // 4] = (packed - 32768).astype(jnp.int16)
+
+
+def decode(k, groups, code_ref, step_ref, value_ref):
+    for low in range(0, groups, 4):
+        packed = code_ref[k, groups + low // 4].astype(jnp.int32) + 32768
+        for g in range(low, min(low + 4, groups)):
+            code = code_ref[k, g].astype(jnp.int32) * 16 + ((packed >> (4 * (g - low))) & 15)
+            value_ref[k, g] = code.astype(F32) * step_ref[k, g]
 
 
 def kernel(
     geometry,
-    coef_ref, chosen_ref, count_ref, x_ref,
-    out_ref, total_ref,
-    recv, own, up_out, up_in, down_out, down_in, tot, ret,
-    cnt_send, cnt, part_send, parts, inverse,
-    x_send_sem, x_recv_sem, r_send_sem, r_recv_sem, z_send_sem, z_recv_sem,
+    table_ref, between_ref, count_ref, x_hbm,
+    out_ref, scale_ref, total_ref,
+    x_ref, recv, own, up_sum, down_sum, up_out, up_in, down_out, down_in,
+    up_out_step, up_in_step, down_out_step, down_in_step, codes, steps, ret, ret_scale,
+    cnt_send, cnt, part_send, parts, inverse, factor,
+    second, third, paths, coef, chosen, load_sem,
+    x_send_sem, x_recv_sem, r_send_sem, r_recv_sem, s_send_sem, s_recv_sem, z_send_sem, z_recv_sem, zs_send_sem, zs_recv_sem,
     c_send_sem, c_recv_sem, p_send_sem, p_recv_sem,
 ):
     across, cols, depth, chunks, wide, groups = geometry
@@ -53,6 +96,8 @@
     def lanes(k):
         return pl.ds(pl.multiple_of(k * wide, 128), wide)
 
+    load = pltpu.make_async_copy(x_hbm, x_ref, load_sem)
+    load.start()
     barrier = pltpu.get_barrier_semaphore()
     for d in range(1, plane):
         pl.semaphore_signal(barrier, inc=1, device_id=member((me + d) % plane), device_id_type=MESH)
@@ -61,6 +106,17 @@
     count = count_ref[0, 0].astype(F32)
     cnt_send[...] = jnp.full(cnt_send.shape, count, F32)
     cnt[me] = jnp.full(cnt_send.shape, count, F32)
+    path_counts(across, cols, z, table_ref, between_ref, second, third, paths, coef, chosen)
+
+    @pl.when(z == 0)
+    def _():
+        up_sum[...] = jnp.zeros(up_sum.shape, F32)
+
+    @pl.when(z == depth - 1)
+    def _():
+        down_sum[...] = jnp.zeros(down_sum.shape, F32)
+
+    load.wait()
     pl.semaphore_wait(barrier, plane + depth - 2)
 
     def count_copy(d):
@@ -97,13 +153,34 @@
             send_sem=r_send_sem.at[k, to], recv_sem=r_recv_sem.at[k, slot],
             device_id=member(to), device_id_type=MESH)
 
+    def scale_copy(k, to, slot):
+        return pltpu.make_async_remote_copy(
+            src_ref=ret_scale.at[k, to], dst_ref=scale_ref.at[slot, :, lanes(k)],
+            send_sem=s_send_sem.at[k, to], recv_sem=s_recv_sem.at[k, slot],
+            device_id=member(to), device_id_type=MESH)
+
     def result_local(k):
         return pltpu.make_async_copy(ret.at[k, me], out_ref.at[me, :, lanes(k)], r_recv_sem.at[k, me])
 
+    def scale_local(k):
+        return pltpu.make_async_copy(ret_scale.at[k, me], scale_ref.at[me, :, lanes(k)], s_recv_sem.at[k, me])
+
+    def up_step_copy(k):
+        return pltpu.make_async_remote_copy(
+            src_ref=up_out_step.at[k], dst_ref=up_in_step.at[k],
+            send_sem=zs_send_sem.at[0, k], recv_sem=zs_recv_sem.at[0, k],
+            device_id=level((z + 1) % depth), device_id_type=MESH)
+
     def up_copy(k):
         return pltpu.make_async_remote_copy(
             src_ref=up_out.at[k], dst_ref=up_in.at[k], send_sem=z_send_sem.at[0, k], recv_sem=z_recv_sem.at[0, k],
             device_id=level((z + 1) % depth), device_id_type=MESH)
+
+    def down_step_copy(k):
+        return pltpu.make_async_remote_copy(
+            src_ref=down_out_step.at[k], dst_ref=down_in_step.at[k],
+            send_sem=zs_send_sem.at[1, k], recv_sem=zs_recv_sem.at[1, k],
+            device_id=level((z + depth - 1) % depth), device_id_type=MESH)
 
     def down_copy(k):
         return pltpu.make_async_remote_copy(
@@ -120,25 +197,16 @@
         def _(d):
             piece_copy(k, (me + d) % plane, me).start()
 
-    @pl.when(z == 0)
-    def _():
-        up_in[...] = jnp.zeros(up_in.shape, F32)
-
-    @pl.when(z == depth - 1)
-    def _():
-        down_in[...] = jnp.zeros(down_in.shape, F32)
-
     @pl.loop(1, plane)
     def _(d):
         count_arrival((me + d) % plane).wait_recv()
 
-    def factor(q, g):
-        return coef_ref[(z * across) * cols + q, g] * cnt[q]
-
     for g in range(groups):
-        part = factor(0, g)
-        for q in range(1, plane):
-            part = part + factor(q, g)
+        part = None
+        for q in range(plane):
+            term = coef[q, g].astype(F32) * cnt[q]
+            factor[q, g] = term
+            part = term if q == 0 else part + term
         part_send[g] = part
         parts[z, g] = part
 
@@ -162,7 +230,7 @@
             for q in range(plane):
                 piece = recv[t, q].astype(F32)
                 for g in range(groups):
-                    term = piece * factor(q, g)
+                    term = piece * factor[q, g]
                     sums[g] = term if q == 0 else sums[g] + term
             for g in range(groups):
                 own[t, g] = sums[g]
@@ -174,10 +242,13 @@
             @pl.when(z > 0)
             def _():
                 up_copy(up).wait_recv()
+                up_step_copy(up).wait_recv()
+                decode(up, groups, up_in, up_in_step, up_sum)
 
             @pl.when(z < depth - 1)
             def _():
-                up_out[up] = own[up] + up_in[up]
+                encode(lambda g: own[up, g] + up_sum[up, g], up, groups, up_out, up_out_step)
+                up_step_copy(up).start()
                 up_copy(up).start()
 
         down = t - SKEW * (depth - 1 - z)
@@ -187,10 +258,13 @@
             @pl.when(z < depth - 1)
             def _():
                 down_copy(down).wait_recv()
+                down_step_copy(down).wait_recv()
+                decode(down, groups, down_in, down_in_step, down_sum)
 
             @pl.when(z > 0)
             def _():
-                down_out[down] = own[down] + down_in[down]
+                encode(lambda g: own[down, g] + down_sum[down, g], down, groups, down_out, down_out_step)
+                down_step_copy(down).start()
                 down_copy(down).start()
 
         end = t - SKEW * far
@@ -207,21 +281,28 @@
                     weight = weight + parts[s, g]
                 parts[z, g] = weight
                 inverse[g] = 1.0 / weight
-            total_ref[...] = parts[z, chosen_ref[row * cols + col]].astype(jnp.int32)
+            total_ref[...] = parts[z, chosen[me], :, :1].astype(jnp.int32)
 
         @pl.when((end >= 0) & (end < chunks))
         def _():
             for g in range(groups):
-                tot[g] = (own[end, g] + up_in[end, g] + down_in[end, g]) * inverse[g]
+                mean = (own[end, g] + up_sum[end, g] + down_sum[end, g]) * inverse[g]
+                step = jnp.maximum(jnp.max(jnp.abs(mean), axis=0, keepdims=True), SMALLEST) * (1.0 / LIMIT)
+                steps[g] = step
+                codes[g] = jnp.round(mean * (1.0 / step)).astype(jnp.int32).astype(jnp.int16)
 
             @pl.loop(1, plane)
             def _(d):
                 to = (me + d) % plane
-                ret[end, to] = tot[chosen_ref[(z * across) * cols + to]]
+                ret[end, to] = codes[chosen[to]]
+                ret_scale[end, to] = steps[chosen[to]]
                 result_copy(end, to, me).start()
-
-            ret[end, me] = tot[chosen_ref[row * cols + col]]
+                scale_copy(end, to, me).start()
+
+            ret[end, me] = codes[chosen[me]]
+            ret_scale[end, me] = steps[chosen[me]]
             result_local(end).start()
+            scale_local(end).start()
 
     @pl.loop(1, plane)
     def _(d):
@@ -236,18 +317,23 @@
         @pl.when(z < depth - 1)
         def _():
             up_copy(k).wait_send()
+            up_step_copy(k).wait_send()
 
         @pl.when(z > 0)
         def _():
             down_copy(k).wait_send()
+            down_step_copy(k).wait_send()
 
         @pl.loop(1, plane)
         def _(d):
             piece_copy(k, (me + d) % plane, me).wait_send()
             result_copy(k, (me + d) % plane, me).wait_send()
             result_copy(k, me, (me + d) % plane).wait_recv()
+            scale_copy(k, (me + d) % plane, me).wait_send()
+            scale_copy(k, me, (me + d) % plane).wait_recv()
 
         result_local(k).wait()
+        scale_local(k).wait()
 
 
 def local(gradients, token_counts, row_groups, col_groups):
@@ -256,42 +342,56 @@
     depth, plane = rows // across, across * cols
     width = gradients.shape[-1]
     height = gradients.size // width // plane
-    wide = 256 if width % 256 == 0 else width
+    wide = WIDE if width % WIDE == 0 else width
     chunks = width // wide
     groups = cols
-    coefficient, chosen = path_counts(row_groups, col_groups)
     pieces = gradients.reshape(plane, height, width)
     smem = pl.BlockSpec(memory_space=pltpu.SMEM)
     vmem = pl.BlockSpec(memory_space=pltpu.VMEM)
     slab = pltpu.VMEM((chunks, groups, height, wide), F32)
+    coded = pltpu.VMEM((chunks, groups + pl.cdiv(groups, 4), height, wide), jnp.int16)
+    step = pltpu.VMEM((chunks, groups, 1, wide), F32)
     sem = pltpu.SemaphoreType.DMA
-    averaged, total = pl.pallas_call(
+    codes, scales, total = pl.pallas_call(
         functools.partial(kernel, (across, cols, depth, chunks, wide, groups)),
         out_shape=(
-            jax.ShapeDtypeStruct((plane, height, width), F32),
-            jax.ShapeDtypeStruct((1, wide), jnp.int32),
+            jax.ShapeDtypeStruct((plane, height, width), jnp.int16),
+            jax.ShapeDtypeStruct((plane, 1, width), F32),
+            jax.ShapeDtypeStruct((1, 1), jnp.int32),
         ),
-        in_specs=[smem, smem, smem, vmem],
-        out_specs=(pl.BlockSpec(memory_space=pl.ANY), vmem),
+        in_specs=[smem, smem, smem, pl.BlockSpec(memory_space=pltpu.HBM)],
+        out_specs=(vmem, vmem, vmem),
         scratch_shapes=[
+            pltpu.VMEM((plane, height, width), gradients.dtype),
             pltpu.VMEM((chunks, plane, height, wide), gradients.dtype),
-            slab, slab, slab, slab, slab,
-            pltpu.VMEM((groups, height, wide), F32),
-            pltpu.VMEM((chunks, plane, height, wide), F32),
+            slab, slab, slab, coded, coded, coded, coded, step, step, step, step,
+            pltpu.VMEM((groups, height, wide), jnp.int16),
+            pltpu.VMEM((groups, 1, wide), F32),
+            pltpu.VMEM((chunks, plane, height, wide), jnp.int16),
+            pltpu.VMEM((chunks, plane, 1, wide), F32),
             pltpu.VMEM((1, wide), F32),
             pltpu.VMEM((plane, 1, wide), F32),
             pltpu.VMEM((groups, 1, wide), F32),
             pltpu.VMEM((depth, groups, 1, wide), F32),
             pltpu.VMEM((groups, 1, wide), F32),
+            pltpu.VMEM((plane, groups, 1, wide), F32),
+            pltpu.SMEM((rows, groups), jnp.int32),
+            pltpu.SMEM((rows, groups), jnp.int32),
+            pltpu.SMEM((groups, groups), jnp.int32),
+            pltpu.SMEM((plane, groups), jnp.int32),
+            pltpu.SMEM((plane,), jnp.int32),
+            sem,
             sem((chunks, plane)), sem((chunks, plane)), sem((chunks, plane)), sem((chunks, plane)),
-            sem((2, chunks)), sem((2, chunks)),
+            sem((chunks, plane)), sem((chunks, plane)),
+            sem((2, chunks)), sem((2, chunks)), sem((2, chunks)), sem((2, chunks)),
             sem((plane,)), sem((plane,)), sem((depth,)), sem((depth,)),
         ],
         compiler_params=pltpu.CompilerParams(
-            collective_id=0, has_side_effects=True, vmem_limit_bytes=48 * 1024 * 1024
+            collective_id=0, has_side_effects=True, vmem_limit_bytes=VMEM_GRANT
         ),
-    )(coefficient, chosen, token_counts, pieces)
-    return averaged.reshape(gradients.shape), total[:, :1]
+    )(jnp.swapaxes(row_groups, 1, 2), col_groups, token_counts, pieces)
+    averaged = codes.astype(F32) * scales
+    return averaged.reshape(gradients.shape), total
 
 
 def solution(mesh):

time: 54.3 us -> 46.6 us (0.86)
  Pallas kernels: 46.9 us -> 39.4 us
  between operations: 1.3 us -> 3.04 us
  local copies, waits for them, and re-layouts: 3.89 us -> 2.5 us
  matrix products: 1.33 us -> 0 us
  other arithmetic: 0.73 us -> 1.42 us
    pallas_call x1, Pallas kernels: 46.9 us -> 39.4 us  [local(): pl.pallas_call(functools.partial(kernel, (across, cols, depth, chunks, wi...]
    mul x0 -> x1, other arithmetic: none -> 1.42 us  [local(): averaged = codes.astype(F32) * scales]
    dot_general x4 -> x0, matrix products: 1.33 us -> none  [the longest x1 0.87 us: path_counts(): to_second = exact('ijh,ijg->hg', between, first)]
    eq x2 -> x0, local copies, waits for them, and re-layouts: 0.82 us -> none  [path_counts(): first = (row_groups[0][:, None, :] == col_ids[None, :, None]).astype(F32)]
    eq x2 -> x0, other arithmetic: 0.7 us -> none  [the longest x1 0.69 us: path_counts(): between = (col_groups[0][None, :, :] == row_ids[:, None, None]).astype(F32)]
    unnamed x3 -> x7, local copies, waits for them, and re-layouts: 2.28 us -> 2.5 us
where the time goes in v2:
time: 46.6 us; the launch traced here: 46.3 us
  Pallas kernels  39.4 us (85%)
  between operations  3.04 us (7%)
  local copies, waits for them, and re-layouts  2.5 us (5%)
  other arithmetic  1.42 us (3%)
    pallas_call x1, Pallas kernels, local(): pl.pallas_call(functools.partial(kernel, (across, cols, depth, chunks, wi...  39.4 us
    unnamed x7, local copies, waits for them, and re-layouts  2.5 us
    mul x1, other arithmetic, local(): averaged = codes.astype(F32) * scales  1.42 us

profile of v2, /device:TPU:0, one launch (start us, length us, event | category | flops | bytes accessed | tf_op | source)
XLA Modules:
  0.0 46.3 jit_solution(10044221153181844894)
XLA Ops:
  1.3 0.0 copy-start
  1.3 1.1 %copy-done = bf16[1,1,4,64,1536]{4,3,2,1,0:T(8,128)(2,1)S(1)} copy-done((bf16[1,1,4,64,1536]{4,3,2,1,0:T(8,128)(2,1)S(1)}, bf16[1,1,4,64,1536]{4,3,2,1,0:T(8,128)(2,1)}, u32[]{:S(2)}) %copy-start) | copy-done | bytes 786456
  2.4 0.0 copy-start.1
  2.4 0.7 %copy-done.1 = s32[2,8,4]{1,2,0:T(4,128)S(1)} copy-done((s32[2,8,4]{1,2,0:T(4,128)S(1)}, s32[2,8,4]{1,2,0:T(4,128)}, u32[]{:S(2)}) %copy-start.1) | copy-done | bytes 280
  3.1 0.0 copy-start.2
  3.1 0.7 %copy-done.2 = s32[1,4,8]{2,1,0:T(4,128)S(1)} copy-done((s32[1,4,8]{2,1,0:T(4,128)S(1)}, s32[1,4,8]{2,1,0:T(4,128)}, u32[]{:S(2)}) %copy-start.2) | copy-done | bytes 152
  3.8 39.4 %shard_map.59 = (s16[8,32,1536]{2,1,0:T(8,128)(2,1)S(1)}, f32[8,1,1536]{2,1,0:T(1,128)S(1)}, s32[1,1]{1,0:T(1,128)}) custom-call(s32[2,4,8]{2,1,0:T(4,128)S(1)} %bitcast.7, s32[1,4,8]{2,1,0:T(4,128)S(1)} %copy-done.2, s32[1,1]{1,0:T(1,128)S(6)} %copy.10.count_ref, bf16[8,32,1536]{2,1,0:T(8,128)(2,1)S(1)} %bitcast.6), custom_call_target="tpu_custom_call" | custom-call | tf_op jit(solution)/shard_map/pallas_call | solution.py:355
  43.2 1.4 %convert_multiply_fusion = f32[8,32,1536]{2,1,0:T(8,128)} fusion(s16[8,32,1536]{2,1,0:T(8,128)(2,1)S(1)} %get-tuple-element.5, f32[8,1536]{1,0:T(8,128)S(1)} %bitcast.9), kind=kLoop, calls=%fused_computation | loop fusion | flops 786432 | bytes 2408448 | tf_op jit(solution)/shard_map/mul | solution.py:393
  (1 shorter events, 0.0 us)
Async XLA Ops:
  1.3 1.1 %copy-start = (bf16[1,1,4,64,1536]{4,3,2,1,0:T(8,128)(2,1)S(1)}, bf16[1,1,4,64,1536]{4,3,2,1,0:T(8,128)(2,1)}, u32[]{:S(2)}) copy-start(bf16[1,1,4,64,1536]{4,3,2,1,0:T(8,128)(2,1)} %param.4) | copy-start | bytes 2359300
  2.4 0.7 %copy-start.1 = (s32[2,8,4]{1,2,0:T(4,128)S(1)}, s32[2,8,4]{1,2,0:T(4,128)}, u32[]{:S(2)}) copy-start(s32[2,8,4]{1,2,0:T(4,128)} %param.6) | copy-start | bytes 772
  3.1 0.7 %copy-start.2 = (s32[1,4,8]{2,1,0:T(4,128)S(1)}, s32[1,4,8]{2,1,0:T(4,128)}, u32[]{:S(2)}) copy-start(s32[1,4,8]{2,1,0:T(4,128)} %between_ref.1) | copy-start | bytes 388

commit v3 on v2

--- a/solution.py
+++ b/solution.py
@@ -72,12 +72,12 @@
 
 def kernel(
     geometry,
-    table_ref, between_ref, count_ref, x_hbm,
+    table_ref, between_ref, count_ref, x_ref,
     out_ref, scale_ref, total_ref,
-    x_ref, recv, own, up_sum, down_sum, up_out, up_in, down_out, down_in,
+    recv, own, up_sum, down_sum, up_out, up_in, down_out, down_in,
     up_out_step, up_in_step, down_out_step, down_in_step, codes, steps, ret, ret_scale,
     cnt_send, cnt, part_send, parts, inverse, factor,
-    second, third, paths, coef, chosen, load_sem,
+    second, third, paths, coef, chosen,
     x_send_sem, x_recv_sem, r_send_sem, r_recv_sem, s_send_sem, s_recv_sem, z_send_sem, z_recv_sem, zs_send_sem, zs_recv_sem,
     c_send_sem, c_recv_sem, p_send_sem, p_recv_sem,
 ):
@@ -96,8 +96,6 @@
     def lanes(k):
         return pl.ds(pl.multiple_of(k * wide, 128), wide)
 
-    load = pltpu.make_async_copy(x_hbm, x_ref, load_sem)
-    load.start()
     barrier = pltpu.get_barrier_semaphore()
     for d in range(1, plane):
         pl.semaphore_signal(barrier, inc=1, device_id=member((me + d) % plane), device_id_type=MESH)
@@ -116,7 +114,6 @@
     def _():
         down_sum[...] = jnp.zeros(down_sum.shape, F32)
 
-    load.wait()
     pl.semaphore_wait(barrier, plane + depth - 2)
 
     def count_copy(d):
@@ -291,7 +288,7 @@
                 steps[g] = step
                 codes[g] = jnp.round(mean * (1.0 / step)).astype(jnp.int32).astype(jnp.int16)
 
-            @pl.loop(1, plane)
+            @pl.loop(1, plane, unroll=True)
             def _(d):
                 to = (me + d) % plane
                 ret[end, to] = codes[chosen[to]]
@@ -359,10 +356,9 @@
             jax.ShapeDtypeStruct((plane, 1, width), F32),
             jax.ShapeDtypeStruct((1, 1), jnp.int32),
         ),
-        in_specs=[smem, smem, smem, pl.BlockSpec(memory_space=pltpu.HBM)],
+        in_specs=[smem, smem, smem, vmem],
         out_specs=(vmem, vmem, vmem),
         scratch_shapes=[
-            pltpu.VMEM((plane, height, width), gradients.dtype),
             pltpu.VMEM((chunks, plane, height, wide), gradients.dtype),
             slab, slab, slab, coded, coded, coded, coded, step, step, step, step,
             pltpu.VMEM((groups, height, wide), jnp.int16),
@@ -380,7 +376,6 @@
             pltpu.SMEM((groups, groups), jnp.int32),
             pltpu.SMEM((plane, groups), jnp.int32),
             pltpu.SMEM((plane,), jnp.int32),
-            sem,
             sem((chunks, plane)), sem((chunks, plane)), sem((chunks, plane)), sem((chunks, plane)),
             sem((chunks, plane)), sem((chunks, plane)),
             sem((2, chunks)), sem((2, chunks)), sem((2, chunks)), sem((2, chunks)),

time: 46.6 us -> 46.5 us (level)
  no operation moved by 1% of the time
where the time goes in v3:
time: 46.5 us; the launch traced here: 46.2 us
  Pallas kernels  39.3 us (85%)
  between operations  3.04 us (7%)
  local copies, waits for them, and re-layouts  2.5 us (5%)
  other arithmetic  1.42 us (3%)
    pallas_call x1, Pallas kernels, local(): pl.pallas_call(functools.partial(kernel, (across, cols, depth, chunks, wi...  39.3 us
    unnamed x7, local copies, waits for them, and re-layouts  2.5 us
    mul x1, other arithmetic, local(): averaged = codes.astype(F32) * scales  1.42 us

profile of v3, /device:TPU:0, one launch (start us, length us, event | category | flops | bytes accessed | tf_op | source)
XLA Modules:
  0.0 46.2 jit_solution(828260648610740588)
XLA Ops:
  1.3 0.0 copy-start
  1.3 1.1 %copy-done = bf16[1,1,4,64,1536]{4,3,2,1,0:T(8,128)(2,1)S(1)} copy-done((bf16[1,1,4,64,1536]{4,3,2,1,0:T(8,128)(2,1)S(1)}, bf16[1,1,4,64,1536]{4,3,2,1,0:T(8,128)(2,1)}, u32[]{:S(2)}) %copy-start) | copy-done | bytes 786456
  2.4 0.0 copy-start.1
  2.4 0.7 %copy-done.1 = s32[2,8,4]{1,2,0:T(4,128)S(1)} copy-done((s32[2,8,4]{1,2,0:T(4,128)S(1)}, s32[2,8,4]{1,2,0:T(4,128)}, u32[]{:S(2)}) %copy-start.1) | copy-done | bytes 280
  3.1 0.0 copy-start.2
  3.1 0.7 %copy-done.2 = s32[1,4,8]{2,1,0:T(4,128)S(1)} copy-done((s32[1,4,8]{2,1,0:T(4,128)S(1)}, s32[1,4,8]{2,1,0:T(4,128)}, u32[]{:S(2)}) %copy-start.2) | copy-done | bytes 152
  3.8 39.3 %shard_map.59 = (s16[8,32,1536]{2,1,0:T(8,128)(2,1)S(1)}, f32[8,1,1536]{2,1,0:T(1,128)S(1)}, s32[1,1]{1,0:T(1,128)}) custom-call(s32[2,4,8]{2,1,0:T(4,128)S(1)} %bitcast.7, s32[1,4,8]{2,1,0:T(4,128)S(1)} %copy-done.2, s32[1,1]{1,0:T(1,128)S(6)} %copy.10.count_ref, bf16[8,32,1536]{2,1,0:T(8,128)(2,1)S(1)} %bitcast.6), custom_call_target="tpu_custom_call" | custom-call | tf_op jit(solution)/shard_map/pallas_call | solution.py:352
  43.1 1.4 %convert_multiply_fusion = f32[8,32,1536]{2,1,0:T(8,128)} fusion(s16[8,32,1536]{2,1,0:T(8,128)(2,1)S(1)} %get-tuple-element.5, f32[8,1536]{1,0:T(8,128)S(1)} %bitcast.9), kind=kLoop, calls=%fused_computation | loop fusion | flops 786432 | bytes 2408448 | tf_op jit(solution)/shard_map/mul | solution.py:388
  (1 shorter events, 0.0 us)
Async XLA Ops:
  1.3 1.1 %copy-start = (bf16[1,1,4,64,1536]{4,3,2,1,0:T(8,128)(2,1)S(1)}, bf16[1,1,4,64,1536]{4,3,2,1,0:T(8,128)(2,1)}, u32[]{:S(2)}) copy-start(bf16[1,1,4,64,1536]{4,3,2,1,0:T(8,128)(2,1)} %param.4) | copy-start | bytes 2359300
  2.4 0.7 %copy-start.1 = (s32[2,8,4]{1,2,0:T(4,128)S(1)}, s32[2,8,4]{1,2,0:T(4,128)}, u32[]{:S(2)}) copy-start(s32[2,8,4]{1,2,0:T(4,128)} %param.6) | copy-start | bytes 772
  3.1 0.7 %copy-start.2 = (s32[1,4,8]{2,1,0:T(4,128)S(1)}, s32[1,4,8]{2,1,0:T(4,128)}, u32[]{:S(2)}) copy-start(s32[1,4,8]{2,1,0:T(4,128)} %between_ref.1) | copy-start | bytes 388
